TPU v7x, 256 devices: a whole 4x4x8 slice. The times are simulated.
256 devices in a mesh: pb: 32 (over z_hi, y, x), row: 8 (over z_lo, core).
Axes of the slice: x: 4, y: 4, z: 8 (z_hi: 2, z_lo: 4; z = z_hi * 4 + z_lo), core: 2. Of those that a mesh axis runs over, the one named last changes fastest.
Arguments:
- screened: bfloat16 [64, 2, 1024, 1024], P('pb', None, 'row'), may hold values from -1.0546875 to 1.0546875
- response: bfloat16 [64, 2, 1024, 1024], P(None, None, 'pb', 'row'), may hold values from -0.1875 to 0.1875
- q_owner: int32 [64], replicated, may hold values from 0 to 63, each once
- g_index: int32 [64, 1024], P('pb'), may hold values from 0 to 1023, each once within a row
Outputs:
- tangent: float32 [64, 2, 1024, 1024], P(None, None, ('row', 'pb'))
Inputs may be any that keep to these rules, and one draw needn't show every extreme that they name: `q_owner`: each owner slot appears once. `g_index`: each row is a permutation of the 1024 plane waves.
All inputs are finite; a program needn't handle non-finite values.
Results may differ from a plain program's by a relative error of at most 0.0029.
Values may be sent and summed in bfloat16 or wider, within the bound.
No kernel may reach another device: no remote copies, remote signals or barrier semaphores. Data moves between devices by JAX's collectives and lax.ppermute only.
A program may use at most 64 MiB of HBM per device.

v0:
```python
import jax
import jax.numpy as jnp
from jax import lax
from jax.sharding import PartitionSpec as P


def split_up(x, dim, length):
    before, after = (x.shape[:dim], x.shape[dim + 1 :])
    return jnp.moveaxis(x.reshape(*before, length, -1, *after), dim, 0)


def cut_rows(length, count):
    unit = 8 if length >= 8 * count else 1
    return [length // unit * k // count * unit for k in range(1, count)]


def laid_out(tiles, dim):
    tiles = jnp.moveaxis(tiles, 0, dim)
    lengths = tiles.shape
    return tiles.reshape(*lengths[:dim], lengths[dim] * lengths[dim + 1], *lengths[dim + 2 :])


def several_exchanges(x, axis, pieces, split_dim, concat_dim):
    tiles = split_up(x, split_dim, lax.axis_size(axis))
    cut = max(range(1, max(2, tiles.ndim - 1)), key=lambda d: tiles.shape[d])
    done = []
    for section in jnp.split(tiles, cut_rows(tiles.shape[cut], pieces), axis=cut):
        if section.size:
            done.append(lax.all_to_all(section, axis, split_axis=0, concat_axis=0, tiled=True))
    return laid_out(jnp.concatenate(done, axis=cut), concat_dim)


def complex_product(left, right):

    def product(first, second):
        return jnp.einsum("qik,qkj->qij", first, second, preferred_element_type=jnp.float32)

    real_part = product(left[:, 0], right[:, 0]) - product(left[:, 1], right[:, 1])
    imag_part = product(left[:, 0], right[:, 1]) + product(left[:, 1], right[:, 0])
    return jnp.stack((real_part, imag_part), axis=1)


def body(screened, response, q_owner, g_index):
    slot_count = q_owner.shape[0]
    inverse = (
        jnp.zeros((slot_count,), jnp.int32).at[q_owner].set(jnp.arange(slot_count, dtype=jnp.int32))
    )
    ordered = jnp.take(response, inverse, axis=0)
    at_owner = several_exchanges(ordered, "pb", 2, 0, 2)
    permuted = jax.vmap(lambda block, table: block[:, table, :])(at_owner, g_index)
    whole = lax.all_gather(screened, "row", axis=2, tiled=True)
    column_half = complex_product(whole, permuted).astype(jnp.bfloat16)
    halfway = lax.all_to_all(column_half, "row", split_axis=2, concat_axis=3, tiled=True)
    result = complex_product(halfway, whole)
    returned = lax.all_to_all(result, "pb", split_axis=2, concat_axis=0, tiled=True)
    return jnp.take(returned, q_owner, axis=0)


def solution(mesh):
    return jax.shard_map(
        body,
        mesh=mesh,
        in_specs=(P("pb", None, "row", None), P(None, None, "pb", "row"), P(), P("pb", None)),
        out_specs=P(None, None, ("row", "pb"), None),
        check_vma=False,
    )
```

profile of v0, /device:TPU:2, one launch (start us, length us, event | category | flops | bytes accessed | tf_op | source)
XLA Modules:
  0.0 260.0 jit_solution(11688914136311840597)
XLA Ops:
  6.5 0.0 copy-start
  6.5 0.0 all-gather.2.cloned.1.call-start
  6.5 2.4 copy.25
  8.9 0.0 all-gather.2.cloned.1.call-update
  8.9 0.7 compare_select_fusion.2
  9.6 0.8 scatter_custom_fusion
  10.4 0.1 broadcast_in_dim.32
  10.5 0.0 copy-done
  10.5 0.0 copy-start.2
  10.5 0.7 gather_fusion
  11.3 0.2 broadcast_select_fusion.1
  11.5 1.1 fusion.25
  12.6 39.0 %all_to_all.46 = bf16[32,2,2,16,128]{4,3,2,1,0:T(8,128)(2,1)S(1)} all-to-all(bf16[32,2,2,16,128]{4,3,2,1,0:T(8,128)(2,1)S(1)} %get-tuple-element.5), channel_id=1, replica_groups=mesh['pb'=32,'row'=8] {'pb'}, dimensions={0} | all-to-all | bytes 1048576 | tf_op jit(solution)/shard_map/all_to_all | solution.py:29
  51.6 5.2 %all-to-all-start.1 = ((bf16[32,2,2,16,128]{4,3,2,1,0:T(8,128)(2,1)}), bf16[32,2,2,16,128]{4,3,2,1,0:T(8,128)(2,1)S(1)}, u32[]{:S(2)}, u32[]{:S(2)}) async-start(bf16[32,2,2,16,128]{4,3,2,1,0:T(8,128)(2,1)} %get-tuple-element.6), calls=%async_computation.1 | async-start | bytes 1048576 | tf_op jit(solution)/shard_map/all_to_all | solution.py:29
  56.8 0.0 copy-done.2
  56.9 23.8 %all-to-all-done.1 = bf16[32,2,2,16,128]{4,3,2,1,0:T(8,128)(2,1)S(1)} async-done(((bf16[32,2,2,16,128]{4,3,2,1,0:T(8,128)(2,1)}), bf16[32,2,2,16,128]{4,3,2,1,0:T(8,128)(2,1)S(1)}, u32[]{:S(2)}, u32[]{:S(2)}) %all-to-all-start.1) | async-done | bytes 524320 | tf_op jit(solution)/shard_map/all_to_all | solution.py:29
  80.7 0.1 maximum_bitcast_fusion
  80.8 0.1 copy.21
  80.9 1.1 copy.22
  82.0 8.5 %gather_fusion.2 = bf16[2048,2,128]{2,1,0:T(2,128)(2,1)S(1)} fusion(bf16[2,2,1024,128]{3,1,2,0:T(2,128)(2,1)S(1)} %copy.22, s32[2048]{0:T(1024)S(1)} %bitcast.90), kind=kCustom, calls=%fused_computation.2 | custom fusion | bytes 2113536 | tf_op jit(solution)/shard_map/vmap()/gather | solution.py:50
  90.5 0.8 copy.24
  91.4 37.1 %all-gather.2.cloned.1.call-done = bf16[2,2,1024,1024]{3,2,0,1:T(8,128)(2,1)} async-done(((bf16[2,2,128,1024]{3,2,0,1:T(8,128)(2,1)}), bf16[2,2,1024,1024]{3,2,0,1:T(8,128)(2,1)}) %all-gather.2.cloned.1.call-update) | async-done | bytes 8388624 | tf_op jit(solution)/shard_map/all_gather | solution.py:51
  128.4 3.9 %fusion.3 = f32[2,128,1024]{2,1,0:T(8,128)S(1)} fusion(bf16[2,2,1024,1024]{3,2,0,1:T(8,128)(2,1)} %all-gather.2.cloned.1.call-done, bf16[2,2,1024,128]{2,3,0,1:T(8,128)(2,1)S(1)} %bitcast.100), kind=kOutput, calls=%fused_computation.9 | convolution fusion | flops 536870912 | bytes 5767168 | tf_op jit(solution)/shard_map/qik,qkj->qij/dot_general | solution.py:36
  132.3 3.7 %fusion.2 = f32[2,128,1024]{2,1,0:T(8,128)S(1)} fusion(bf16[2,2,1024,1024]{3,2,0,1:T(8,128)(2,1)} %all-gather.2.cloned.1.call-done, bf16[2,2,1024,128]{2,3,0,1:T(8,128)(2,1)S(1)} %bitcast.101), kind=kOutput, calls=%fused_computation.8 | convolution fusion | flops 536870912 | bytes 5767168 | tf_op jit(solution)/shard_map/qik,qkj->qij/dot_general | solution.py:36
  136.0 0.0 copy-done.1
  136.0 1.5 fusion.16
  137.5 1.5 fusion.17
  139.1 0.1 pad_maximum_fusion.1
  139.2 0.9 copy.26
  140.0 29.0 %all_to_all.47 = bf16[2,2,1024,128]{3,0,1,2:T(2,128)(2,1)S(1)} all-to-all(bf16[2,2,1024,128]{3,0,1,2:T(2,128)(2,1)S(1)} %copy.26), channel_id=1, replica_groups=mesh['pb'=32,'row'=8] {'row'}, dimensions={2} | all-to-all | bytes 2097152 | tf_op jit(solution)/shard_map/all_to_all | solution.py:53
  169.0 0.7 copy.35
  169.7 0.5 all_to_all.37
  170.2 0.0 slice-start
  170.2 3.1 %fusion.1 = f32[2,128,1024]{2,1,0:T(8,128)S(1)} fusion(bf16[2,2,1024,1024]{3,2,0,1:T(8,128)(2,1)} %all-gather.2.cloned.1.call-done, bf16[2,2,128,1024]{3,2,0,1:T(8,128)(2,1)S(1)} %all_to_all.37), kind=kOutput, calls=%fused_computation.7 | convolution fusion | flops 536870912 | bytes 5767168 | tf_op jit(solution)/shard_map/qik,qkj->qij/dot_general | solution.py:36
  173.3 0.0 slice-start.1
  173.3 3.1 %fusion = f32[2,128,1024]{2,1,0:T(8,128)S(1)} fusion(bf16[2,2,1024,1024]{3,2,0,1:T(8,128)(2,1)} %all-gather.2.cloned.1.call-done, bf16[2,2,128,1024]{3,2,0,1:T(8,128)(2,1)S(1)} %all_to_all.37), kind=kOutput, calls=%fused_computation.6 | convolution fusion | flops 536870912 | bytes 5767168 | tf_op jit(solution)/shard_map/qik,qkj->qij/dot_general | solution.py:36
  176.4 3.0 %fusion.11 = f32[2,1,128,1024]{3,2,0,1:T(8,128)S(1)} fusion(f32[2,128,1024]{2,1,0:T(8,128)S(1)} %fusion.1, bf16[2,2,1024,1024]{3,2,0,1:T(8,128)(2,1)} %all-gather.2.cloned.1.call-done, bf16[2,2,128,1024]{3,2,0,1:T(8,128)(2,1)S(1)} %all_to_all.37), kind=kOutput, calls=%fused_computation.18 | convolution fusion | flops 537133056 | bytes 6815744 | tf_op jit(solution)/shard_map/qik,qkj->qij/dot_general | solution.py:36
  179.3 0.0 slice-done
  179.3 0.7 fusion.13
  180.1 0.1 pad_maximum_fusion
  180.3 0.0 copy-start.3
  180.3 2.9 %copy.28 = f32[2,2,128,1024]{3,0,1,2:T(2,128)} copy(f32[2,2,128,1024]{3,2,0,1:T(8,128)S(1)} %pad_maximum_fusion) | data formatting | bytes 4194304 | tf_op jit(solution)/shard_map/stack | solution.py:40
  183.2 11.4 %all-to-all-start.3 = ((f32[2,2,128,1024]{3,0,1,2:T(2,128)}), f32[2,2,128,1024]{3,0,1,2:T(2,128)S(1)}, u32[]{:S(2)}, u32[]{:S(2)}) async-start(f32[2,2,128,1024]{3,0,1,2:T(2,128)} %copy.28), calls=%async_computation.3 | async-start | bytes 4194304 | tf_op jit(solution)/shard_map/all_to_all | solution.py:55
  194.6 0.0 copy-done.3
  194.6 50.2 %all-to-all-done.3 = f32[2,2,128,1024]{3,0,1,2:T(2,128)S(1)} async-done(((f32[2,2,128,1024]{3,0,1,2:T(2,128)}), f32[2,2,128,1024]{3,0,1,2:T(2,128)S(1)}, u32[]{:S(2)}, u32[]{:S(2)}) %all-to-all-start.3) | async-done | bytes 2097184 | tf_op jit(solution)/shard_map/all_to_all | solution.py:55
  244.8 3.1 %copy.29 = f32[2,2,32,4,1024]{4,3,1,0,2:T(4,128)} copy(f32[2,2,32,4,1024]{4,0,1,3,2:T(2,128)S(1)} %bitcast.91) | data formatting | bytes 4194304 | tf_op jit(solution)/shard_map/all_to_all | solution.py:55
  247.9 3.4 %gather_fusion.1 = f32[64,2,4,1024]{3,2,1,0:T(4,128)S(1)} fusion(f32[64,2,4,1024]{3,2,1,0:T(4,128)} %bitcast.92, s32[1024]{0:T(1024)S(1)} %pad_clamp_fusion), kind=kCustom, calls=%fused_computation.1 | custom fusion | bytes 4194560 | tf_op jit(solution)/shard_map/jit(_take)/gather | solution.py:56
  251.3 1.8 broadcast_select_fusion
  (11 shorter events, 0.1 us)
Async XLA Ops:
  6.5 4.0 %copy-start = (bf16[64,2,32,128]{3,2,1,0:T(8,128)(2,1)S(1)}, bf16[64,2,32,128]{3,2,1,0:T(8,128)(2,1)}, u32[]{:S(2)}) copy-start(bf16[64,2,32,128]{3,2,1,0:T(8,128)(2,1)} %param.5) | copy-start | bytes 3145732
  6.5 121.9 %all-gather.2.cloned.1.call-start = ((), (), s32[]{:S(2)}) async-start(), calls=%async_computation.4 | async-start | bytes 9437184 | tf_op jit(solution)/shard_map/all_gather | solution.py:51
  10.5 46.3 %copy-start.2 = (s32[2,1024]{1,0:T(2,128)S(1)}, s32[2,1024]{1,0:T(2,128)}, u32[]{:S(2)}) copy-start(s32[2,1024]{1,0:T(2,128)} %param.7) | copy-start | bytes 24580
  51.6 29.1 %all-to-all-start.1 = ((bf16[32,2,2,16,128]{4,3,2,1,0:T(8,128)(2,1)}), bf16[32,2,2,16,128]{4,3,2,1,0:T(8,128)(2,1)S(1)}, u32[]{:S(2)}, u32[]{:S(2)}) async-start(bf16[32,2,2,16,128]{4,3,2,1,0:T(8,128)(2,1)} %get-tuple-element.6), calls=%async_computation.1 | async-start | bytes 1048576 | tf_op jit(solution)/shard_map/all_to_all | solution.py:29
  128.4 7.6 %copy-start.1 = (bf16[2,2,1024,1024]{3,2,0,1:T(8,128)(2,1)S(1)}, bf16[2,2,1024,1024]{3,2,0,1:T(8,128)(2,1)}, u32[]{:S(2)}) copy-start(bf16[2,2,1024,1024]{3,2,0,1:T(8,128)(2,1)} %all-gather.2.cloned.1.call-done) | copy-start | bytes 25165828
  170.2 9.1 %slice-start = ((s8[8388608]{0:T(1024)(128)(4,1)}), s8[4194304]{0:T(1024)(128)(4,1)S(1)}, s32[]{:S(2)}) async-start(s8[8388608]{0:T(1024)(128)(4,1)} %bitcast.93), calls=%async_computation.5 | async-start | bytes 8388608
  173.3 6.1 %slice-start.1 = ((s8[8388608]{0:T(1024)(128)(4,1)}), s8[4194304]{0:T(1024)(128)(4,1)S(1)}, s32[]{:S(2)}) async-start(s8[8388608]{0:T(1024)(128)(4,1)} %bitcast.93), calls=%async_computation.6 | async-start | bytes 8388608
  180.3 14.3 %copy-start.3 = (s32[64]{0:T(128)S(1)}, s32[64]{0:T(128)}, u32[]{:S(2)}) copy-start(s32[64]{0:T(128)} %param.6) | copy-start | bytes 772
  183.2 61.6 %all-to-all-start.3 = ((f32[2,2,128,1024]{3,0,1,2:T(2,128)}), f32[2,2,128,1024]{3,0,1,2:T(2,128)S(1)}, u32[]{:S(2)}, u32[]{:S(2)}) async-start(f32[2,2,128,1024]{3,0,1,2:T(2,128)} %copy.28), calls=%async_computation.3 | async-start | bytes 4194304 | tf_op jit(solution)/shard_map/all_to_all | solution.py:55
Sparse Core Ops, SparseCore 0:
  9.1 119.2 all-gather.1
where the time goes:
time: 260 us
  waiting for transfers between devices  111 us (43%)
  blocking collectives  68 us (26%)
  local copies, waits for them, and re-layouts  27.1 us (10%)
  matrix products  20.4 us (8%)
  starting transfers between devices  16.6 us (6%)
  between operations  13.7 us (5%)
  other arithmetic  3.08 us (1%)
    all_to_all x1, waiting for transfers between devices, body(): lax.all_to_all(result, 'pb', split_axis=2, concat_axis=0, tiled=True)  50.2 us
    all_to_all x1, blocking collectives, several_exchanges(): lax.all_to_all(section, axis, split_axis=0, concat_axis=0, tiled=True)  39 us
    all_gather x1, waiting for transfers between devices, body(): whole = lax.all_gather(screened, 'row', axis=2, tiled=True)  37.1 us
    all_to_all x1, blocking collectives, body(): lax.all_to_all(column_half, 'row', split_axis=2, concat_axis=3, tiled=True)  29 us
    all_to_all x1, waiting for transfers between devices, several_exchanges(): lax.all_to_all(section, axis, split_axis=0, concat_axis=0, tiled=True)  23.8 us
    dot_general x8, matrix products, product(): jnp.einsum('qik,qkj->qij', first, second, preferred_element_type=jnp.floa...  20.4 us
    all_to_all x1, starting transfers between devices, body(): lax.all_to_all(result, 'pb', split_axis=2, concat_axis=0, tiled=True)  11.4 us
    gather x2, local copies, waits for them, and re-layouts, body(): block[:, table, :]  9.35 us
  transfers between devices with their start and end apart: 3, of which 3 were waited for; matrix products, arithmetic and copies ran while one was open for 5% of the time, Pallas kernels for 0%

commit v1 on v0

v1 whole, which is shorter than its diff:
```python
import jax
import jax.numpy as jnp
from jax import lax
from jax.sharding import Mesh, PartitionSpec as P

OWNER = ("zh", "y", "x")
ROW = ("zm", "zn", "c")
SPREAD = ("zh", "y", "x", "zm")


def swap(x, axes, mask=None):
    count = 2 ** len(axes)
    mask = count - 1 if mask is None else mask
    return lax.ppermute(x, axes, [(i, i ^ mask) for i in range(count)])


def complex_product(left, right):
    def product(first, second):
        return jnp.dot(first, second, preferred_element_type=jnp.float32)

    real_part = product(left[0], right[0]) - product(left[1], right[1])
    imag_part = product(left[0], right[1]) + product(left[1], right[0])
    return jnp.stack((real_part, imag_part))


def body(screened, response, q_owner, g_index):
    slots = q_owner.shape[0]
    _, parts, rows, size = screened.shape
    zm = lax.axis_index("zm")

    def pick(x, k, axis=0):
        return lax.dynamic_index_in_dim(x, k, axis, keepdims=False)

    mine = pick(screened, zm)
    other = swap(pick(screened, 1 - zm), ("zm",))
    pair = jnp.stack((mine, other))
    four = jnp.stack((pair, swap(pair, ("zn",))))
    whole = jnp.stack((four, swap(four, ("c",))))
    weight = jnp.moveaxis(whole, 3, 0).reshape(parts, size, size)

    ids = jnp.arange(slots, dtype=jnp.int32)
    inverse = jnp.sum(jnp.where(q_owner[None, :] == ids[:, None], ids[None, :], 0), axis=1)
    ordered = jnp.take(response, inverse, axis=0)
    landed = lax.all_to_all(ordered, SPREAD, 0, 0, tiled=True)
    short, columns = landed.shape[2:]
    landed = landed.reshape(slots // 2, 2, parts, short, columns)
    chi = jnp.stack((pick(landed, zm, 1), pick(landed, 1 - zm, 1)), axis=3)
    chi = jnp.moveaxis(chi, 1, 0).reshape(parts, size, 2 * columns)
    table = pick(g_index, zm)
    choose = (table[:, None] == jnp.arange(size, dtype=jnp.int32)[None, :]).astype(jnp.bfloat16)
    chi = jnp.einsum("ik,pkj->pij", choose, chi, preferred_element_type=jnp.float32)
    chi = chi.astype(jnp.bfloat16)

    half = complex_product(weight, chi).astype(jnp.bfloat16)
    blocks = half.reshape(parts, 2, 2, 2 * rows, 2 * columns)
    got = [
        blocks[:, 0, 0],
        swap(blocks[:, 0, 1], ("zn",)),
        swap(blocks[:, 1, 0], ("c",)),
        swap(blocks[:, 1, 1], ("zn", "c")),
    ]
    half = jnp.concatenate(got, axis=2)

    result = complex_product(half, weight).astype(jnp.bfloat16)
    own = slots // 2
    result = result.reshape(parts, 2, own, rows // own, size)
    result = jnp.stack((pick(result, zm, 1), pick(result, 1 - zm, 1)), axis=0)
    result = jnp.moveaxis(result, 2, 0)
    result = result.reshape(slots, parts, rows // own, size)
    returned = lax.all_to_all(result, SPREAD, 0, 0, tiled=True)
    return jnp.take(returned, q_owner, axis=0).astype(jnp.float32)


def solution(mesh):
    split = Mesh(mesh.devices.reshape(2, 4, 4, 2, 2, 2), OWNER + ROW)
    return jax.shard_map(
        body,
        mesh=split,
        in_specs=(P(OWNER, None, ROW, None), P(None, None, OWNER, ROW), P(), P(OWNER, None)),
        out_specs=P(None, None, ROW + OWNER, None),
        check_vma=False,
    )
```

time: 260 us -> 164 us (0.63)
  blocking collectives: 68 us -> 0 us
  waiting for transfers between devices: 111 us -> 95.7 us
  between operations: 13.7 us -> 0.24 us
  local copies, waits for them, and re-layouts: 27.1 us -> 14.6 us
  starting transfers between devices: 16.6 us -> 27.4 us
  other arithmetic: 3.08 us -> 11.3 us
  matrix products: 20.4 us -> 12.7 us
    all_to_all x2 -> x0, blocking collectives: 68 us -> none  [the longest x1 39 us: several_exchanges(): lax.all_to_all(section, axis, split_axis=0, concat_axis=0, tiled=True)]
    ppermute x0 -> x6, waiting for transfers between devices: none -> 47.3 us  [swap(): return lax.ppermute(x, axes, [(i, i ^ mask) for i in range(count)])]
    all_gather x1 -> x0, waiting for transfers between devices: 37.1 us -> none  [body(): whole = lax.all_gather(screened, 'row', axis=2, tiled=True)]
    all_to_all x2, waiting for transfers between devices: 74 us -> 48.4 us  [the longest x1 29 us: body(): returned = lax.all_to_all(result, SPREAD, 0, 0, tiled=True)]
    gather x3 -> x1, local copies, waits for them, and re-layouts: 12.7 us -> 1.44 us  [body(): return jnp.take(returned, q_owner, axis=0).astype(jnp.float32)]
    dot_general x8 -> x9, matrix products: 20.4 us -> 12.7 us  [the longest x8 9.94 us: product(): return jnp.dot(first, second, preferred_element_type=jnp.float32)]
    ppermute x0 -> x6, starting transfers between devices: none -> 6.31 us  [swap(): return lax.ppermute(x, axes, [(i, i ^ mask) for i in range(count)])]
    another operation x2 -> x3, other arithmetic: 0.24 us -> 5.93 us  [the longest x1 3.14 us: body(): whole = jnp.stack((four, swap(four, ('c',))))]
  transfers between devices with their start and end apart: 3 -> 8, of which waited for: 3 -> 6; matrix products, arithmetic and copies ran while one was open for 5% -> 9% of each run, Pallas kernels for 0% -> 0%
where the time goes in v1:
time: 164 us; the launch traced here: 162 us
  waiting for transfers between devices  95.7 us (58%)
  starting transfers between devices  27.4 us (17%)
  local copies, waits for them, and re-layouts  14.6 us (9%)
  matrix products  12.7 us (8%)
  other arithmetic  11.3 us (7%)
    ppermute x6, waiting for transfers between devices, swap(): return lax.ppermute(x, axes, [(i, i ^ mask) for i in range(count)])  47.3 us
    all_to_all x1, waiting for transfers between devices, body(): returned = lax.all_to_all(result, SPREAD, 0, 0, tiled=True)  29 us
    all_to_all x1, waiting for transfers between devices, body(): landed = lax.all_to_all(ordered, SPREAD, 0, 0, tiled=True)  19.4 us
    all_to_all x1, starting transfers between devices, body(): landed = lax.all_to_all(ordered, SPREAD, 0, 0, tiled=True)  13.6 us
    dot_general x8, matrix products, product(): return jnp.dot(first, second, preferred_element_type=jnp.float32)  9.94 us
    all_to_all x1, starting transfers between devices, body(): returned = lax.all_to_all(result, SPREAD, 0, 0, tiled=True)  7.45 us
    ppermute x6, starting transfers between devices, swap(): return lax.ppermute(x, axes, [(i, i ^ mask) for i in range(count)])  6.31 us
    another operation x3, local copies, waits for them, and re-layouts, complex_product(): return jnp.stack((real_part, imag_part))  3.56 us
  transfers between devices with their start and end apart: 8, of which 6 were waited for; matrix products, arithmetic and copies ran while one was open for 9% of the time, Pallas kernels for 0%

profile of v1, /device:TPU:2, one launch (start us, length us, event | category | flops | bytes accessed | tf_op | source)
XLA Modules:
  0.0 161.9 jit_solution(10183147107548240170)
XLA Ops:
  0.0 1.4 constant_dynamic-slice_fusion.3
  1.4 3.4 %collective-permute-start = (bf16[2,128,1024]{2,1,0:T(8,128)(2,1)S(1)}, bf16[2,128,1024]{2,1,0:T(8,128)(2,1)S(1)}, u32[]{:S(2)}, u32[]{:S(2)}) collective-permute-start(bf16[2,128,1024]{2,1,0:T(8,128)(2,1)S(1)} %get-tuple-element.20), channel_id=1, source_target_pairs={{0,4},{4,0},{1,5},{5,1},{2,6},{6,2},{3,7},{7,3},{8,12},{12,8},{9,1... | collective-permute-start | bytes 1572872 | tf_op jit(solution)/shard_map/ppermute | solution.py:14
  4.8 0.1 select_reduce_fusion
  4.9 23.0 %collective-permute-done = bf16[2,128,1024]{2,1,0:T(8,128)(2,1)S(1)} collective-permute-done((bf16[2,128,1024]{2,1,0:T(8,128)(2,1)S(1)}, bf16[2,128,1024]{2,1,0:T(8,128)(2,1)S(1)}, u32[]{:S(2)}, u32[]{:S(2)}) %collective-permute-start) | collective-permute-done | bytes 524320 | tf_op jit(solution)/shard_map/ppermute | solution.py:14
  27.9 1.1 fusion.26
  29.1 0.7 collective-permute-start.1
  29.8 0.7 gather_fusion
  30.6 1.2 broadcast_select_fusion
  31.7 13.6 %all-to-all-start = ((bf16[64,2,32,128]{3,2,1,0:T(8,128)(2,1)}), bf16[64,2,32,128]{3,2,1,0:T(8,128)(2,1)}, u32[]{:S(2)}, u32[]{:S(2)}) async-start(bf16[64,2,32,128]{3,2,1,0:T(8,128)(2,1)} %broadcast_select_fusion), calls=%async_computation | async-start | bytes 2097152 | tf_op jit(solution)/shard_map/all_to_all | solution.py:44
  45.4 15.5 %collective-permute-done.1 = bf16[2,2,128,1024]{3,2,1,0:T(8,128)(2,1)} collective-permute-done((bf16[2,2,128,1024]{3,2,1,0:T(8,128)(2,1)S(1)}, bf16[2,2,128,1024]{3,2,1,0:T(8,128)(2,1)}, u32[]{:S(2)}, u32[]{:S(2)}) %collective-permute-start.1) | collective-permute-done | bytes 1048608 | tf_op jit(solution)/shard_map/ppermute | solution.py:14
  60.8 3.1 %fusion.27 = (bf16[1,2,2,2,128,1024]{5,4,3,2,1,0:T(8,128)(2,1)S(1)}, bf16[2,2,2,128,1024]{4,3,2,1,0:T(8,128)(2,1)}) fusion(bf16[1,2,2,128,1024]{4,3,2,1,0:T(8,128)(2,1)} %bitcast.3, bf16[1,2,2,128,1024]{4,3,2,1,0:T(8,128)(2,1)} %get-tuple-element.17), kind=kLoop, calls=%fused_computation.68 | loop fusion | flops 1048576 | bytes 6291456 | tf_op jit(solution)/shard_map/stack | solution.py:38
  64.0 0.0 collective-permute-start.2
  64.0 19.4 %all-to-all-done = bf16[64,2,32,128]{3,2,1,0:T(8,128)(2,1)} async-done(((bf16[64,2,32,128]{3,2,1,0:T(8,128)(2,1)}), bf16[64,2,32,128]{3,2,1,0:T(8,128)(2,1)}, u32[]{:S(2)}, u32[]{:S(2)}) %all-to-all-start) | async-done | bytes 1048608 | tf_op jit(solution)/shard_map/all_to_all | solution.py:44
  83.3 1.3 dynamic-slice_bitcast_fusion.1
  84.6 0.1 maximum_bitcast_fusion.1
  84.7 2.1 %copy.32 = bf16[2,32,32,2,128]{4,3,2,1,0:T(2,128)(2,1)} copy(bf16[2,32,32,2,128]{4,2,0,1,3:T(8,128)(2,1)S(1)} %maximum_bitcast_fusion.1) | data formatting | bytes 2097152 | tf_op jit(solution)/shard_map/transpose | solution.py:48
  86.8 2.5 %reshape.59 = bf16[2,1024,256]{2,1,0:T(8,128)(2,1)} reshape(bf16[2,32,32,2,128]{4,3,2,1,0:T(2,128)(2,1)} %copy.32) | data formatting | bytes 2097152 | tf_op jit(solution)/shard_map/reshape | solution.py:48
  89.3 2.7 %fusion.7 = bf16[2,1024,256]{1,2,0:T(8,128)(2,1)S(1)} fusion(bf16[2,1024,256]{2,1,0:T(8,128)(2,1)} %reshape.59, s32[1024]{0:T(1024)S(1)} %bitcast.93), kind=kOutput, calls=%fused_computation.9 | convolution fusion | flops 1075314688 | bytes 2101248 | tf_op jit(solution)/shard_map/ik,pkj->pij/dot_general | solution.py:51
  92.0 0.0 collective-permute-done.2
  92.0 2.0 %maximum_bitcast_fusion = bf16[2,2,2,2,128,1024]{5,4,0,3,2,1:T(8,128)(2,1)S(1)} fusion(bf16[1,2,2,2,128,1024]{5,4,3,2,1,0:T(8,128)(2,1)} %bitcast.5, bf16[1,2,2,2,128,1024]{5,4,3,2,1,0:T(8,128)(2,1)S(1)} %get-tuple-element.7), kind=kLoop, calls=%fused_computation.2 | loop fusion | flops 2097152 | bytes 8388608 | tf_op jit(solution)/shard_map/transpose | solution.py:39
  94.0 0.4 fusion.28
  94.4 0.7 fusion.14
  95.2 0.7 fusion.15
  95.9 0.8 fusion.11
  96.7 0.8 fusion.10
  97.5 0.1 fusion.21
  97.6 1.6 %collective-permute-start.3 = (bf16[2,256,256]{2,1,0:T(8,128)(2,1)S(1)}, bf16[2,256,256]{2,1,0:T(8,128)(2,1)S(1)}, u32[]{:S(2)}, u32[]{:S(2)}) collective-permute-start(bf16[2,256,256]{2,1,0:T(8,128)(2,1)S(1)} %get-tuple-element.12), channel_id=1, source_target_pairs={{0,2},{2,0},{1,3},{3,1},{4,6},{6,4},{5,7},{7,5},{8,10},{10,8},{9,1... | collective-permute-start | bytes 786440 | tf_op jit(solution)/shard_map/ppermute | solution.py:14
  99.3 0.0 collective-permute-start.4
  99.3 0.6 collective-permute-start.5
  99.8 6.1 %collective-permute-done.3 = bf16[2,256,256]{2,1,0:T(8,128)(2,1)S(1)} collective-permute-done((bf16[2,256,256]{2,1,0:T(8,128)(2,1)S(1)}, bf16[2,256,256]{2,1,0:T(8,128)(2,1)S(1)}, u32[]{:S(2)}, u32[]{:S(2)}) %collective-permute-start.3) | collective-permute-done | bytes 262176 | tf_op jit(solution)/shard_map/ppermute | solution.py:14
  105.9 0.0 collective-permute-done.4
  105.9 2.8 %collective-permute-done.5 = bf16[2,256,256]{2,1,0:T(8,128)(2,1)S(1)} collective-permute-done((bf16[2,256,256]{2,1,0:T(8,128)(2,1)S(1)}, bf16[2,256,256]{2,1,0:T(8,128)(2,1)S(1)}, u32[]{:S(2)}, u32[]{:S(2)}) %collective-permute-start.5) | collective-permute-done | bytes 262176 | tf_op jit(solution)/shard_map/ppermute | solution.py:14
  108.7 0.1 pad_maximum_fusion.2
  108.8 0.7 fusion.16
  109.5 1.7 %fusion.17 = f32[256,1024]{1,0:T(8,128)} fusion(bf16[1024,1024]{1,0:T(8,128)(2,1)S(1)} %bitcast.88, bf16[2,256,1024]{2,1,0:T(8,128)(2,1)S(1)} %pad_maximum_fusion.2), kind=kOutput, calls=%fused_computation.42 | convolution fusion | flops 536870912 | bytes 3670016 | tf_op jit(solution)/shard_map/dot_general | solution.py:19
  111.2 1.6 fusion.13
  112.8 2.0 %stack.76 = bf16[1,2,32,4,1024]{4,3,2,1,0:T(4,128)(2,1)} reshape(bf16[256,1024]{1,0:T(8,128)(2,1)} %fusion.13) | data formatting | bytes 1048576 | tf_op jit(solution)/shard_map/stack | solution.py:23
  114.8 2.9 %fusion.12 = bf16[256,1024]{1,0:T(8,128)(2,1)} fusion(f32[256,1024]{1,0:T(8,128)} %fusion.17, bf16[1024,1024]{1,0:T(8,128)(2,1)S(1)} %bitcast.85, bf16[2,256,1024]{2,1,0:T(8,128)(2,1)} %copy-done.1), kind=kOutput, calls=%fused_computation.22 | convolution fusion | flops 537395200 | bytes 4194304 | tf_op jit(solution)/shard_map/dot_general | solution.py:19
  117.8 1.3 stack.75
  119.1 0.2 constant_dynamic-update-slice_fusion.1
  119.3 0.2 constant_dynamic-update-slice_fusion
  119.5 0.4 constant_dynamic-slice_fusion
  119.9 0.6 copy_bitcast_fusion
  120.5 1.7 %pad_maximum_fusion.3 = bf16[2,2,32,4,1024]{4,3,1,0,2:T(4,128)(2,1)} fusion(bf16[1,2,32,4,1024]{4,3,1,0,2:T(4,128)(2,1)S(1)} %get-tuple-element.21, bf16[1,2,32,4,1024]{4,3,1,0,2:T(4,128)(2,1)S(1)} %get-tuple-element.22), kind=kLoop, calls=%fused_computation.27 | loop fusion | flops 524288 | bytes 2097152 | tf_op jit(solution)/shard_map/stack | solution.py:67
  122.1 7.4 %all-to-all-start.1 = ((bf16[64,2,4,1024]{3,2,1,0:T(4,128)(2,1)}), bf16[64,2,4,1024]{3,2,1,0:T(4,128)(2,1)S(1)}, u32[]{:S(2)}, u32[]{:S(2)}) async-start(bf16[64,2,4,1024]{3,2,1,0:T(4,128)(2,1)} %bitcast.31), calls=%async_computation.1 | async-start | bytes 2097152 | tf_op jit(solution)/shard_map/all_to_all | solution.py:70
  129.6 29.0 %all-to-all-done.1 = bf16[64,2,4,1024]{3,2,1,0:T(4,128)(2,1)S(1)} async-done(((bf16[64,2,4,1024]{3,2,1,0:T(4,128)(2,1)}), bf16[64,2,4,1024]{3,2,1,0:T(4,128)(2,1)S(1)}, u32[]{:S(2)}, u32[]{:S(2)}) %all-to-all-start.1) | async-done | bytes 1048608 | tf_op jit(solution)/shard_map/all_to_all | solution.py:70
  158.7 1.4 gather_fusion.1
  160.1 1.8 %select_convert_fusion = f32[64,2,4,1024]{3,2,1,0:T(4,128)} fusion(bf16[64,2,4,1024]{3,2,1,0:T(4,128)(2,1)S(1)} %gather_fusion.1, pred[64]{0:T(512)(128)(4,1)S(1)} %compare_and_fusion.1), kind=kLoop, calls=%fused_computation.28 | loop fusion | flops 1048576 | bytes 3145792 | tf_op jit(solution)/shard_map/convert_element_type | solution.py:71
  (17 shorter events, 0.1 us)
Async XLA Ops:
  0.0 29.8 %copy-start = (bf16[64,2,32,128]{3,2,1,0:T(8,128)(2,1)S(1)}, bf16[64,2,32,128]{3,2,1,0:T(8,128)(2,1)}, u32[]{:S(2)}) copy-start(bf16[64,2,32,128]{3,2,1,0:T(8,128)(2,1)} %param.5) | copy-start | bytes 3145732
  0.0 4.8 %copy-start.4 = (s32[64]{0:T(128)S(1)}, s32[64]{0:T(128)}, u32[]{:S(2)}) copy-start(s32[64]{0:T(128)} %param.6) | copy-start | bytes 772
  1.4 26.5 %collective-permute-start = (bf16[2,128,1024]{2,1,0:T(8,128)(2,1)S(1)}, bf16[2,128,1024]{2,1,0:T(8,128)(2,1)S(1)}, u32[]{:S(2)}, u32[]{:S(2)}) collective-permute-start(bf16[2,128,1024]{2,1,0:T(8,128)(2,1)S(1)} %get-tuple-element.20), channel_id=1, source_target_pairs={{0,4},{4,0},{1,5},{5,1},{2,6},{6,2},{3,7},{7,3},{8,12},{12,8},{9,1... | collective-permute-start | bytes 1572872 | tf_op jit(solution)/shard_map/ppermute | solution.py:14
  29.1 31.8 %collective-permute-start.1 = (bf16[2,2,128,1024]{3,2,1,0:T(8,128)(2,1)S(1)}, bf16[2,2,128,1024]{3,2,1,0:T(8,128)(2,1)}, u32[]{:S(2)}, u32[]{:S(2)}) collective-permute-start(bf16[2,2,128,1024]{3,2,1,0:T(8,128)(2,1)S(1)} %get-tuple-element.18), channel_id=1, source_target_pairs={{0,2},{2,0},{1,3},{3,1},{4,6},{6,4},{5,7},{7,5},{8,10},{10,8},{9,1... | collective-permute-start | bytes 3145736 | tf_op jit(solution)/shard_map/ppermute | solution.py:14
  31.7 51.6 %all-to-all-start = ((bf16[64,2,32,128]{3,2,1,0:T(8,128)(2,1)}), bf16[64,2,32,128]{3,2,1,0:T(8,128)(2,1)}, u32[]{:S(2)}, u32[]{:S(2)}) async-start(bf16[64,2,32,128]{3,2,1,0:T(8,128)(2,1)} %broadcast_select_fusion), calls=%async_computation | async-start | bytes 2097152 | tf_op jit(solution)/shard_map/all_to_all | solution.py:44
  60.8 3.2 %copy-start.3 = (s32[2,1024]{1,0:T(2,128)S(1)}, s32[2,1024]{1,0:T(2,128)}, u32[]{:S(2)}) copy-start(s32[2,1024]{1,0:T(2,128)} %param.7) | copy-start | bytes 24580
  64.0 28.0 %collective-permute-start.2 = (bf16[2,2,2,128,1024]{4,3,2,1,0:T(8,128)(2,1)}, bf16[2,2,2,128,1024]{4,3,2,1,0:T(8,128)(2,1)}, u32[]{:S(2)}, u32[]{:S(2)}) collective-permute-start(bf16[2,2,2,128,1024]{4,3,2,1,0:T(8,128)(2,1)} %get-tuple-element.8), channel_id=1, source_target_pairs={{0,1},{1,0},{2,3},{3,2},{4,5},{5,4},{6,7},{7,6},{8,9},{9,8},{10,11... | collective-permute-start | bytes 6291464 | tf_op jit(solution)/shard_map/ppermute | solution.py:14
  97.6 8.3 %collective-permute-start.3 = (bf16[2,256,256]{2,1,0:T(8,128)(2,1)S(1)}, bf16[2,256,256]{2,1,0:T(8,128)(2,1)S(1)}, u32[]{:S(2)}, u32[]{:S(2)}) collective-permute-start(bf16[2,256,256]{2,1,0:T(8,128)(2,1)S(1)} %get-tuple-element.12), channel_id=1, source_target_pairs={{0,2},{2,0},{1,3},{3,1},{4,6},{6,4},{5,7},{7,5},{8,10},{10,8},{9,1... | collective-permute-start | bytes 786440 | tf_op jit(solution)/shard_map/ppermute | solution.py:14
  99.3 6.6 %collective-permute-start.4 = (bf16[2,256,256]{2,1,0:T(8,128)(2,1)S(1)}, bf16[2,256,256]{2,1,0:T(8,128)(2,1)S(1)}, u32[]{:S(2)}, u32[]{:S(2)}) collective-permute-start(bf16[2,256,256]{2,1,0:T(8,128)(2,1)S(1)} %get-tuple-element.14), channel_id=1, source_target_pairs={{0,1},{1,0},{2,3},{3,2},{4,5},{5,4},{6,7},{7,6},{8,9},{9,8},{10,11... | collective-permute-start | bytes 786440 | tf_op jit(solution)/shard_map/ppermute | solution.py:14
  99.3 9.4 %collective-permute-start.5 = (bf16[2,256,256]{2,1,0:T(8,128)(2,1)S(1)}, bf16[2,256,256]{2,1,0:T(8,128)(2,1)S(1)}, u32[]{:S(2)}, u32[]{:S(2)}) collective-permute-start(bf16[2,256,256]{2,1,0:T(8,128)(2,1)S(1)} %get-tuple-element.13), channel_id=1, source_target_pairs={{0,3},{1,2},{2,1},{3,0},{4,7},{5,6},{6,5},{7,4},{8,11},{9,10},{10,... | collective-permute-start | bytes 786440 | tf_op jit(solution)/shard_map/ppermute | solution.py:14
  108.8 2.4 %copy-start.1 = (bf16[2,256,1024]{2,1,0:T(8,128)(2,1)}, bf16[2,256,1024]{2,1,0:T(8,128)(2,1)S(1)}, u32[]{:S(2)}) copy-start(bf16[2,256,1024]{2,1,0:T(8,128)(2,1)S(1)} %pad_maximum_fusion.2) | copy-start | bytes 3145732
  117.8 1.5 copy-start.2
  122.1 36.5 %all-to-all-start.1 = ((bf16[64,2,4,1024]{3,2,1,0:T(4,128)(2,1)}), bf16[64,2,4,1024]{3,2,1,0:T(4,128)(2,1)S(1)}, u32[]{:S(2)}, u32[]{:S(2)}) async-start(bf16[64,2,4,1024]{3,2,1,0:T(4,128)(2,1)} %bitcast.31), calls=%async_computation.1 | async-start | bytes 2097152 | tf_op jit(solution)/shard_map/all_to_all | solution.py:70
